TPU v7x, 256 devices: a whole 4x4x8 slice. The times are simulated.
256 devices in a mesh: row: 32 (over z_hi, y, x), col: 8 (over z_lo, core).
Axes of the slice: x: 4, y: 4, z: 8 (z_hi: 2, z_lo: 4; z = z_hi * 4 + z_lo), core: 2. Of those that a mesh axis runs over, the one named last changes fastest.
Arguments:
- w_integral: bfloat16 [38400, 4800], P('row', 'col'), may hold values from -0.125 to 0.125
- amplitudes: bfloat16 [4800, 4800], P('row', 'col'), may hold values from -6 to 6
- task_tiles: int32 [32, 7], P('row'), may hold values from -1 to 7, as said below
Outputs:
- residual: bfloat16 [38400, 4800], P('row', 'col')
Inputs may be any that keep to these rules, and one draw needn't show every extreme that they name: `task_tiles`: in each row block the live entries come first, name distinct contraction tiles, and number 1 to 7; the remaining entries are -1. Some row block has 7 live entries, and row blocks 2 m and 2 m + 1 together have exactly 8.
All inputs are finite; a program needn't handle non-finite values.
Results may differ from a plain program's by a relative error of at most 0.001.
Values may be sent and summed in bfloat16 or wider, within the bound.
No kernel may reach another device: no remote copies, remote signals or barrier semaphores. Data moves between devices by JAX's collectives and lax.ppermute only.
A program may use at most 128 MiB of HBM per device.

v0:
```python
import jax
import jax.numpy as jnp
from jax import lax
from jax.sharding import Mesh
from jax.sharding import PartitionSpec as P

TILE = 24
OCC_BLK = 25
MOST = 7
ROW = ("row_0", "row_1", "row_2")


def in_order(pieces, dim):
    pieces = jnp.moveaxis(pieces, 0, dim)
    dims = pieces.shape
    return pieces.reshape(*dims[:dim], dims[dim] * dims[dim + 1], *dims[dim + 2 :])


def all_blocks(array, axes, sequence):
    pieces = array
    for k in sequence:
        pieces = lax.all_gather(pieces, axes[k])
    done = sequence[::-1]
    back = [done.index(k) for k in range(len(axes))]
    pieces = pieces.transpose(*back, *range(len(axes), pieces.ndim))
    return pieces.reshape(-1, *array.shape)


def gathered_by_axis(array, axes, sequence, dim):
    return in_order(all_blocks(array, axes, sequence), dim)


def body(w_integral, amplitudes, task_tiles):
    row_panel = lax.all_gather(w_integral, "col", axis=1, tiled=True)
    tile_width = OCC_BLK * TILE
    own_list = task_tiles[0]
    block_rows = row_panel.shape[0]
    zeros_block = jnp.zeros((block_rows, amplitudes.shape[1]), jnp.float32)
    column_panel = gathered_by_axis(amplitudes, ROW, (0, 1, 2), 0)
    cycle_term = zeros_block
    for slot_index in range(MOST):
        tile_id = own_list[slot_index]
        first_col = jnp.maximum(tile_id, 0) * tile_width
        weights = lax.dynamic_slice_in_dim(row_panel, first_col, tile_width, 1)
        product_weights = weights * (tile_id >= 0).astype(jnp.bfloat16)
        first_row = jnp.maximum(tile_id, 0) * tile_width
        tile_rows = lax.dynamic_slice_in_dim(column_panel, first_row, tile_width, 0)
        cycle_term = cycle_term + jnp.dot(
            product_weights, tile_rows, preferred_element_type=jnp.float32
        )
    return cycle_term.astype(jnp.bfloat16)


def solution(mesh):
    torus = Mesh(
        mesh.devices.reshape(2, 4, 4, mesh.shape["col"]), ("row_0", "row_1", "row_2", "col")
    )
    return jax.shard_map(
        body,
        mesh=torus,
        in_specs=(P(ROW, "col"), P(ROW, "col"), P(ROW, None)),
        out_specs=P(ROW, "col"),
        check_vma=False,
    )
```

profile of v0, /device:TPU:2, one launch (start us, length us, event | category | flops | bytes accessed | tf_op | source)
XLA Modules:
  0.0 282.4 jit_solution(960141207314290983)
XLA Ops:
  6.5 0.0 copy-start.2
  6.5 0.0 all-gather.10.cloned.1.call-start
  6.5 17.7 %all-gather.3 = bf16[2,150,600]{2,1,0:T(8,128)(2,1)} all-gather(bf16[1,150,600]{2,1,0:T(8,128)(2,1)} %bitcast.21), channel_id=2, replica_groups=mesh['row_0'=2,'row_1'=4,'row_2'=4,'col'=8] {'row_0'}, dimensions={0}, use_global_device_ids=true | all-gather | bytes 540000 | tf_op jit(solution)/shard_map/all_gather | solution.py:22
  24.2 0.0 all-gather.10.cloned.1.call-update
  24.2 0.0 all-gather.12.cloned.1.call-start
  24.3 29.6 %all-gather.10.cloned.1.call-done = bf16[8,150,600]{2,1,0:T(8,128)(2,1)} async-done(((bf16[2,150,600]{2,1,0:T(8,128)(2,1)}), bf16[8,150,600]{2,1,0:T(8,128)(2,1)}) %all-gather.10.cloned.1.call-update) | async-done | bytes 1440016 | tf_op jit(solution)/shard_map/all_gather | solution.py:22
  53.9 3.7 %copy.6 = bf16[4,2,150,600]{3,1,2,0:T(2,128)(2,1)} copy(bf16[4,2,150,600]{3,2,1,0:T(8,128)(2,1)} %bitcast.20) | data formatting | bytes 2880000 | tf_op jit(solution)/shard_map/all_gather | solution.py:22
  57.6 0.0 copy-start.3
  57.6 0.0 all-gather.12.cloned.1.call-update
  57.6 0.0 all-gather.8.cloned.1.call-start
  57.7 0.0 copy-done.2
  57.7 2.2 copy.5
  59.9 0.0 all-gather.8.cloned.1.call-update
  59.9 0.0 copy-done.3
  59.9 0.7 fusion.37
  69.5 54.9 %all-gather.12.cloned.1.call-done = bf16[16,2,150,600]{3,1,2,0:T(2,128)(2,1)} async-done(((bf16[4,2,150,600]{3,1,2,0:T(2,128)(2,1)}), bf16[16,2,150,600]{3,1,2,0:T(2,128)(2,1)}) %all-gather.12.cloned.1.call-update) | async-done | bytes 5760016 | tf_op jit(solution)/shard_map/all_gather | solution.py:22
  124.4 3.5 %copy.7 = bf16[16,2,150,600]{3,2,1,0:T(8,128)(2,1)S(1)} copy(bf16[16,2,150,600]{3,1,2,0:T(2,128)(2,1)} %all-gather.12.cloned.1.call-done) | data formatting | bytes 11520000 | tf_op jit(solution)/shard_map/all_gather | solution.py:22
  128.0 3.1 %copy.8 = bf16[2,4,4,150,600]{4,3,2,1,0:T(8,128)(2,1)} copy(bf16[2,4,4,150,600]{4,3,0,1,2:T(8,128)(2,1)S(1)} %bitcast.19) | data formatting | bytes 11520000 | tf_op jit(solution)/shard_map/transpose | solution.py:25
  131.1 8.8 %reshape_reshape.3 = bf16[4800,600]{1,0:T(8,128)(2,1)} reshape(bf16[2,4,4,150,600]{4,3,2,1,0:T(8,128)(2,1)} %copy.8) | data formatting | bytes 11520000 | tf_op jit(solution)/shard_map/reshape;reshape | solution.py:16
  139.9 117.8 %all-gather.8.cloned.1.call-done = bf16[1200,4800]{0,1:T(8,128)(2,1)} async-done(((bf16[1200,600]{0,1:T(8,128)(2,1)}), bf16[1200,4800]{0,1:T(8,128)(2,1)}) %all-gather.8.cloned.1.call-update) | async-done | bytes 11520016 | tf_op jit(solution)/shard_map/all_gather | solution.py:34
  257.7 0.0 copy-start
  257.7 3.4 %fusion.13 = f32[1200,600]{1,0:T(8,128)S(1)} fusion(bf16[1200,4800]{0,1:T(8,128)(2,1)} %all-gather.8.cloned.1.call-done, s32[]{:T(128)S(6)} %select_n.28, bf16[4800,600]{1,0:T(8,128)(2,1)} %reshape_reshape.3, bf16[]{:T(256)} %bitcast.1), kind=kOutput, calls=%fused_computation.19 | convolution fusion | flops 866880000 | bytes 5185536 | tf_op jit(solution)/shard_map/dot_general | solution.py:48
  261.1 0.0 copy-done
  261.1 0.0 copy-start.1
  261.1 3.3 %convolution_add_fusion.5 = f32[1200,600]{1,0:T(8,128)S(1)} fusion(f32[1200,600]{1,0:T(8,128)S(1)} %fusion.13, bf16[1200,4800]{0,1:T(8,128)(2,1)} %all-gather.8.cloned.1.call-done, s32[]{:T(128)S(6)} %select_n.29, bf16[4800,600]{1,0:T(8,128)(2,1)S(1)} %copy-done, bf16[]{:T(256)} %bitcast.7), kind=kOutput, calls=%fused_computation.5 | convolution fusion | flops 867600000 | bytes 8257536 | tf_op jit(solution)/shard_map/dot_general | solution.py:48
  264.4 1.7 copy-done.1
  266.0 1.7 convolution_add_fusion.4
  267.8 1.7 convolution_add_fusion.3
  269.5 1.7 convolution_add_fusion.2
  271.2 1.7 convolution_add_fusion.1
  273.0 2.9 %fusion = bf16[1200,600]{1,0:T(8,128)(2,1)} fusion(f32[1200,600]{1,0:T(8,128)S(1)} %convolution_add_fusion.1, bf16[1200,4800]{0,1:T(8,128)(2,1)S(1)} %copy-done.1, s32[]{:T(128)S(6)} %select_n.34, bf16[4800,600]{1,0:T(8,128)(2,1)S(1)} %copy-done, bf16[]{:T(256)} %bitcast.17), kind=kOutput, calls=%fused_computation.6 | convolution fusion | flops 868320000 | bytes 6817026 | tf_op jit(solution)/shard_map/dot_general | solution.py:48
Async XLA Ops:
  6.5 51.2 %copy-start.2 = (bf16[1200,600]{1,0:T(8,128)(2,1)S(1)}, bf16[1200,600]{1,0:T(8,128)(2,1)}, u32[]{:S(2)}) copy-start(bf16[1200,600]{1,0:T(8,128)(2,1)} %param.3) | copy-start | bytes 4320004
  6.5 47.4 %all-gather.10.cloned.1.call-start = ((), (), s32[]{:S(2)}) async-start(), calls=%async_computation.1 | async-start | bytes 1945600 | tf_op jit(solution)/shard_map/all_gather | solution.py:22
  24.2 100.2 %all-gather.12.cloned.1.call-start = ((), (), s32[]{:S(2)}) async-start(), calls=%async_computation.2 | async-start | bytes 7680000 | tf_op jit(solution)/shard_map/all_gather | solution.py:22
  57.6 2.3 copy-start.3
  57.6 200.0 %all-gather.8.cloned.1.call-start = ((), (), s32[]{:S(2)}) async-start(), calls=%async_computation | async-start | bytes 13824000 | tf_op jit(solution)/shard_map/all_gather | solution.py:34
  257.7 3.4 %copy-start = (bf16[4800,600]{1,0:T(8,128)(2,1)S(1)}, bf16[4800,600]{1,0:T(8,128)(2,1)}, u32[]{:S(2)}) copy-start(bf16[4800,600]{1,0:T(8,128)(2,1)} %reshape_reshape.3) | copy-start | bytes 17280004
  261.1 5.0 %copy-start.1 = (bf16[1200,4800]{0,1:T(8,128)(2,1)S(1)}, bf16[1200,4800]{0,1:T(8,128)(2,1)}, u32[]{:S(2)}) copy-start(bf16[1200,4800]{0,1:T(8,128)(2,1)} %all-gather.8.cloned.1.call-done) | copy-start | bytes 34560004
Sparse Core Ops, SparseCore 0:
  24.4 29.4 all-gather.9
  57.8 66.6 all-gather.11
  126.2 131.3 all-gather.7
where the time goes:
time: 283 us; the launch traced here: 282 us
  waiting for transfers between devices  202 us (71%)
  local copies, waits for them, and re-layouts  23.8 us (8%)
  between operations  22.1 us (8%)
  blocking collectives  17.7 us (6%)
  matrix products  16.4 us (6%)
    all_gather x1, waiting for transfers between devices, body(): row_panel = lax.all_gather(w_integral, 'col', axis=1, tiled=True)  118 us
    all_gather x2, waiting for transfers between devices, all_blocks(): pieces = lax.all_gather(pieces, axes[k])  84.5 us
    all_gather x1, blocking collectives, all_blocks(): pieces = lax.all_gather(pieces, axes[k])  17.7 us
    dot_general x7, matrix products, body(): jnp.dot(product_weights, tile_rows, preferred_element_type=jnp.float32)  16.4 us
    another operation x1, local copies, waits for them, and re-layouts, in_order(): pieces.reshape(*dims[:dim], dims[dim] * dims[dim + 1], *dims[dim + 2:])  8.82 us
    all_gather x2, local copies, waits for them, and re-layouts, all_blocks(): pieces = lax.all_gather(pieces, axes[k])  7.26 us
  transfers between devices with their start and end apart: 3, of which 3 were waited for; matrix products, arithmetic and copies ran while one was open for 7% of the time, Pallas kernels for 0%

commit v1 on v0

--- a/solution.py
+++ b/solution.py
@@ -31,7 +31,9 @@
 
 
 def body(w_integral, amplitudes, task_tiles):
-    row_panel = lax.all_gather(w_integral, "col", axis=1, tiled=True)
+    row_panel = jnp.concatenate(
+        lax.all_to_all(jnp.stack(lax.psum(1, "col") * [w_integral]), "col", 0, 0), axis=1
+    )
     tile_width = OCC_BLK * TILE
     own_list = task_tiles[0]
     block_rows = row_panel.shape[0]

time: 283 us -> 381 us (1.35)
  blocking collectives: 17.7 us -> 214 us
  waiting for transfers between devices: 202 us -> 85.5 us
  matrix products: 16.4 us -> 23.2 us
  starting transfers between devices: 0.09 us -> 6.12 us
  local copies, waits for them, and re-layouts: 23.8 us -> 27.9 us
    all_gather x1, blocking collectives: 17.7 us -> 214 us  [all_blocks(): pieces = lax.all_gather(pieces, axes[k])]
    all_gather x1 -> x0, waiting for transfers between devices: 118 us -> none  [body(): row_panel = lax.all_gather(w_integral, 'col', axis=1, tiled=True)]
    dot_general x7, matrix products: 16.4 us -> 23.2 us  [body(): jnp.dot(product_weights, tile_rows, preferred_element_type=jnp.float32)]
    all_to_all x0 -> x1, starting transfers between devices: none -> 6.03 us  [body(): lax.all_to_all(jnp.stack(lax.psum(1, 'col') * [w_integral]), 'col', 0, 0)]
    another operation x0 -> x1, local copies, waits for them, and re-layouts: none -> 5.16 us  [body(): jnp.stack(lax.psum(1, 'col') * [w_integral])]
  transfers between devices with their start and end apart: 3 -> 3, of which waited for: 3 -> 2; matrix products, arithmetic and copies ran while one was open for 7% -> 5% of each run, Pallas kernels for 0% -> 0%
where the time goes in v1:
time: 381 us; the launch traced here: 379 us
  blocking collectives  214 us (56%)
  waiting for transfers between devices  85.5 us (22%)
  local copies, waits for them, and re-layouts  27.9 us (7%)
  matrix products  23.2 us (6%)
  between operations  22.3 us (6%)
  starting transfers between devices  6.12 us (2%)
    all_gather x1, blocking collectives, all_blocks(): pieces = lax.all_gather(pieces, axes[k])  214 us
    all_gather x2, waiting for transfers between devices, all_blocks(): pieces = lax.all_gather(pieces, axes[k])  85.5 us
    dot_general x7, matrix products, body(): jnp.dot(product_weights, tile_rows, preferred_element_type=jnp.float32)  23.2 us
    another operation x1, local copies, waits for them, and re-layouts, in_order(): pieces.reshape(*dims[:dim], dims[dim] * dims[dim + 1], *dims[dim + 2:])  8.82 us
  transfers between devices with their start and end apart: 3, of which 2 were waited for; matrix products, arithmetic and copies ran while one was open for 5% of the time, Pallas kernels for 0%

profile of v1, /device:TPU:2, one launch (start us, length us, event | category | flops | bytes accessed | tf_op | source)
XLA Modules:
  0.0 379.0 jit_solution(11959506298937321476)
XLA Ops:
  6.5 2.7 copy.7
  9.2 5.2 %stack.2 = bf16[8,1200,600]{1,2,0:T(8,128)(2,1)} broadcast(bf16[1200,600]{0,1:T(8,128)(2,1)S(1)} %copy.7), dimensions={1,2} | broadcast | bytes 12960000 | tf_op jit(solution)/shard_map/stack | solution.py:35
  14.4 0.0 copy-start.1
  14.4 6.0 %all-to-all-start = ((bf16[8,1200,600]{1,2,0:T(8,128)(2,1)}), bf16[8,1200,600]{1,2,0:T(8,128)(2,1)}, u32[]{:S(2)}, u32[]{:S(2)}) async-start(bf16[8,1200,600]{1,2,0:T(8,128)(2,1)} %stack.2), calls=%async_computation | async-start | bytes 24576000 | tf_op jit(solution)/shard_map/all_to_all | solution.py:35
  20.4 0.0 copy-start.2
  20.4 0.0 all-gather.7.cloned.1.call-start
  20.5 0.0 copy-done.1
  20.5 214.0 %all-gather.3 = bf16[2,150,600]{2,1,0:T(8,128)(2,1)} all-gather(bf16[1,150,600]{2,1,0:T(8,128)(2,1)S(1)} %bitcast.24), channel_id=2, replica_groups=mesh['row_0'=2,'row_1'=4,'row_2'=4,'col'=8] {'row_0'}, dimensions={0}, use_global_device_ids=true | all-gather | bytes 540000 | tf_op jit(solution)/shard_map/all_gather | solution.py:22
  234.5 0.0 all-gather.7.cloned.1.call-update
  234.5 0.0 all-gather.9.cloned.1.call-start
  234.5 28.2 %all-gather.7.cloned.1.call-done = bf16[8,150,600]{2,1,0:T(8,128)(2,1)} async-done(((bf16[2,150,600]{2,1,0:T(8,128)(2,1)}), bf16[8,150,600]{2,1,0:T(8,128)(2,1)}) %all-gather.7.cloned.1.call-update) | async-done | bytes 1440016 | tf_op jit(solution)/shard_map/all_gather | solution.py:22
  262.8 3.7 copy.8
  266.5 0.0 all-gather.9.cloned.1.call-update
  266.5 0.0 copy-done.2
  266.5 0.7 fusion.37
  276.0 57.2 %all-gather.9.cloned.1.call-done = bf16[16,2,150,600]{3,1,2,0:T(2,128)(2,1)} async-done(((bf16[4,2,150,600]{3,1,2,0:T(2,128)(2,1)}), bf16[16,2,150,600]{3,1,2,0:T(2,128)(2,1)}) %all-gather.9.cloned.1.call-update) | async-done | bytes 5760016 | tf_op jit(solution)/shard_map/all_gather | solution.py:22
  333.3 3.5 copy.9
  336.8 3.2 copy.10
  340.1 8.8 %reshape_reshape.3 = bf16[4800,600]{1,0:T(8,128)(2,1)} reshape(bf16[2,4,4,150,600]{4,3,2,1,0:T(8,128)(2,1)} %copy.10) | data formatting | bytes 11520000 | tf_op jit(solution)/shard_map/reshape;reshape | solution.py:16
  348.9 0.0 all-to-all-done
  348.9 0.0 copy-start
  348.9 3.4 fusion.13
  352.3 0.0 copy-done
  352.3 3.1 convolution_add_fusion.5
  355.5 3.1 convolution_add_fusion.4
  358.6 3.1 convolution_add_fusion.3
  361.7 3.1 convolution_add_fusion.2
  364.8 3.1 convolution_add_fusion.1
  367.9 4.3 %fusion = bf16[1200,600]{1,0:T(8,128)(2,1)} fusion(f32[1200,600]{1,0:T(8,128)S(1)} %convolution_add_fusion.1, bf16[1200,4800]{0,1:T(8,128)(2,1)} %bitcast.1, s32[]{:T(128)S(6)} %select_n.34, bf16[4800,600]{1,0:T(8,128)(2,1)S(1)} %copy-done, bf16[]{:T(256)} %bitcast.20), kind=kOutput, calls=%fused_computation.6 | convolution fusion | flops 868320000 | bytes 6817536 | tf_op jit(solution)/shard_map/dot_general | solution.py:50
Async XLA Ops:
  14.4 6.1 %copy-start.1 = (bf16[150,600]{1,0:T(8,128)(2,1)S(1)}, bf16[150,600]{1,0:T(8,128)(2,1)}, u32[]{:S(2)}) copy-start(bf16[150,600]{1,0:T(8,128)(2,1)} %param.4) | copy-start | bytes 540004
  14.4 334.5 %all-to-all-start = ((bf16[8,1200,600]{1,2,0:T(8,128)(2,1)}), bf16[8,1200,600]{1,2,0:T(8,128)(2,1)}, u32[]{:S(2)}, u32[]{:S(2)}) async-start(bf16[8,1200,600]{1,2,0:T(8,128)(2,1)} %stack.2), calls=%async_computation | async-start | bytes 24576000 | tf_op jit(solution)/shard_map/all_to_all | solution.py:35
  20.4 246.1 %copy-start.2 = (s32[1,7]{1,0:T(1,128)S(1)}, s32[1,7]{1,0:T(1,128)}, u32[]{:S(2)}) copy-start(s32[1,7]{1,0:T(1,128)} %param.5) | copy-start | bytes 88
  20.4 242.3 %all-gather.7.cloned.1.call-start = ((), (), s32[]{:S(2)}) async-start(), calls=%async_computation.1 | async-start | bytes 1945600 | tf_op jit(solution)/shard_map/all_gather | solution.py:22
  234.5 98.8 %all-gather.9.cloned.1.call-start = ((), (), s32[]{:S(2)}) async-start(), calls=%async_computation.2 | async-start | bytes 7680000 | tf_op jit(solution)/shard_map/all_gather | solution.py:22
  348.9 3.4 copy-start
Sparse Core Ops, SparseCore 0:
  234.6 28.1 all-gather.6
  266.6 66.6 all-gather.8
